TPU v7x, 512 devices: a whole 4x8x8 slice. The times are simulated.
512 devices in a mesh: lat: 16 (over y_lo, z), lon: 32 (over x, y_hi, core).
Axes of the slice: x: 4, y: 8 (y_hi: 4, y_lo: 2; y = y_hi * 2 + y_lo), z: 8, core: 2. Of those that a mesh axis runs over, the one named last changes fastest.
Arguments:
- tokens: bfloat16 [384, 256, 768], P('lat', 'lon'), may hold values from -6 to 6
- gain_zonal: float32 [768], replicated, may hold values from 0.25 to 1.75
- qkv_zonal: bfloat16 [768, 2304], P('lat'), may hold values from -1 to 1
- out_zonal: bfloat16 [768, 768], P('lat'), may hold values from -0.21875 to 0.21875
- gain_merid: float32 [768], replicated, may hold values from 0.25 to 1.75
- qkv_merid: bfloat16 [768, 2304], P('lat'), may hold values from -1 to 1
- out_merid: bfloat16 [768, 768], P('lat'), may hold values from -0.21875 to 0.21875
Outputs:
- result: bfloat16 [384, 256, 768], P('lat', 'lon')
All inputs are finite; a program needn't handle non-finite values.
Results may differ from a plain program's by a relative error of at most 0.0095.
Values may be sent and summed in bfloat16 or wider, within the bound.
A program may use at most 64 MiB of HBM per device.

v0:
```python
import jax
import jax.numpy as jnp
from jax import lax
from jax.sharding import Mesh
from jax.sharding import PartitionSpec as P

HEADS = 12
HEAD_DIM = 64
LON = ("lon_0", "lon_1", "lon_2")


def side_by_side(arrays, axis, dim, along):
    ends, at = ([], 0)
    for a in arrays[:-1]:
        at += a.shape[along]
        ends.append(at)
    both = jnp.concatenate(arrays, axis=along)
    return tuple(jnp.split(lax.all_gather(both, axis, axis=dim, tiled=True), ends, axis=along))


def grouped_exchange(array, axis, split_dim, concat_dim, work, item_dim, out_dim):

    def moved(group):
        return lax.all_to_all(group, axis, split_axis=split_dim, concat_axis=concat_dim, tiled=True)

    items = jax.tree.leaves(array)[0].shape[item_dim]
    ends = [items * k // 2 for k in range(2 + 1)] if items % 2 == 0 else [0, items]
    groups = [
        jax.tree.map(lambda a: lax.slice_in_dim(a, low, high, axis=item_dim), array)
        for low, high in zip(ends, ends[1:])
    ]
    arrived = [moved(group) for group in groups]
    made = [work(group) for group in arrived]
    return jax.tree.map(lambda *parts: jnp.concatenate(parts, axis=out_dim), *made)


def cut_along(array, dim, count):
    shape = array.shape
    parts = array.reshape(*shape[:dim], count, shape[dim] // count, *shape[dim + 1 :])
    return jnp.moveaxis(parts, dim, 0)


def joined_along(parts, dim):
    shape = list(parts.shape[1:])
    shape[dim] *= parts.shape[0]
    return jnp.moveaxis(parts, 0, dim).reshape(shape)


def turned_blocks(parts, axes, sequence):
    shape = [lax.axis_size(a) for a in axes]
    parts = parts.reshape(*shape, *parts.shape[1:])
    for k in sequence:
        parts = lax.all_to_all(parts, axes[k], split_axis=k, concat_axis=k, tiled=True)
    return parts.reshape(-1, *parts.shape[len(axes) :])


def exchange_by_chip(array, groups, sequence, split_dim, concat_dim):
    count = lax.axis_size(groups[0]) * lax.axis_size(groups[1])
    parts = cut_along(array, split_dim, count)
    return joined_along(turned_blocks(parts, groups, sequence), concat_dim)


def normalize(values, gain):
    wide = values.astype(jnp.float32)
    factor = lax.rsqrt(jnp.mean(wide * wide, axis=-1, keepdims=True) + 1e-05)
    return (wide * factor * gain).astype(jnp.bfloat16)


def group_size(count, length):
    target = max(1, -(-512 // length))
    chosen = 1
    for option in range(1, count + 1):
        if count % option == 0 and option <= target:
            chosen = option
    return chosen


def attend_items(packed):
    leading, count, length, triple = packed.shape
    total = leading * count
    width = triple // 3
    group = group_size(total, length)
    blocks = packed.reshape(total // group, group, length, 3, width)

    def one_block(block):
        scores = jnp.einsum(
            "gqe,gke->gqk", block[:, :, 0], block[:, :, 1], preferred_element_type=jnp.float32
        ) * HEAD_DIM ** (-0.5)
        ceiling = jnp.max(scores, axis=-1, keepdims=True)
        powers = jnp.exp(scores - ceiling)
        weights = (powers / jnp.sum(powers, axis=-1, keepdims=True)).astype(jnp.bfloat16)
        mixed = jnp.einsum(
            "gqk,gke->gqe", weights, block[:, :, 2], preferred_element_type=jnp.float32
        )
        return mixed.astype(jnp.bfloat16)

    outputs = lax.map(one_block, blocks)
    return outputs.reshape(leading, count, length, width)


def split_heads(normed, projection, form):
    shaped = projection.reshape(projection.shape[0], 3, HEADS, HEAD_DIM)
    return jnp.einsum(form, normed, shaped, preferred_element_type=jnp.float32).astype(jnp.bfloat16)


def residual_add(base, mixed, mixer, form):
    shaped = mixer.reshape(HEADS, HEAD_DIM, mixer.shape[1])
    update = jnp.einsum(form, mixed, shaped, preferred_element_type=jnp.float32)
    return (base.astype(jnp.float32) + update).astype(jnp.bfloat16)


def fetch_pair(projection, mixer):
    whole = side_by_side((projection, mixer), "lat", 0, 1)
    return whole


def body(tokens, gain_zonal, qkv_zonal, out_zonal, gain_merid, qkv_merid, out_merid):
    rows_here, cols_here, _ = tokens.shape
    lon_count = lax.axis_size(LON)
    lat_count = lax.axis_size("lat")
    zonal_project, zonal_mixer = fetch_pair(qkv_zonal, out_zonal)
    normed_zonal = normalize(tokens, gain_zonal)
    zonal_packed = split_heads(normed_zonal, zonal_project, "rcd,dthe->rhcte")
    zonal_packed = zonal_packed.reshape(
        lon_count, rows_here * HEADS // lon_count, cols_here, 3 * HEAD_DIM
    )
    zonal_mixed = grouped_exchange(zonal_packed, LON, 0, 2, attend_items, 1, 1)
    zonal_home = exchange_by_chip(zonal_mixed, (("lon_0", "lon_1"), "lon_2"), (1, 0), 2, 0)
    zonal_home = zonal_home.reshape(rows_here, HEADS, cols_here, HEAD_DIM)
    after_zonal = residual_add(tokens, zonal_home, zonal_mixer, "rhce,hef->rcf")
    merid_pair = fetch_pair(qkv_merid, out_merid)
    normed_merid = normalize(after_zonal, gain_merid)
    merid_packed = split_heads(normed_merid, merid_pair[0], "rcd,dthe->chrte")
    merid_packed = merid_packed.reshape(
        lat_count, cols_here * HEADS // lat_count, rows_here, 3 * HEAD_DIM
    )
    merid_mixed = attend_items(
        lax.all_to_all(merid_packed, "lat", split_axis=0, concat_axis=2, tiled=True)
    )
    merid_home = lax.all_to_all(merid_mixed, "lat", split_axis=2, concat_axis=0, tiled=True)
    merid_home = merid_home.reshape(cols_here, HEADS, rows_here, HEAD_DIM)
    return residual_add(after_zonal, merid_home, merid_pair[1], "chre,hef->rcf")


def solution(mesh):
    finer = Mesh(
        mesh.devices.reshape(mesh.shape["lat"], 4, 4, 2), ("lat", "lon_0", "lon_1", "lon_2")
    )
    return jax.shard_map(
        body,
        mesh=finer,
        in_specs=(
            P("lat", LON, None),
            P(),
            P("lat", None),
            P("lat", None),
            P(),
            P("lat", None),
            P("lat", None),
        ),
        out_specs=P("lat", LON, None),
        check_vma=False,
    )
```

profile of v0, /device:TPU:1, one launch (start us, length us, event | category | flops | bytes accessed | tf_op | source)
XLA Modules:
  0.0 286.5 jit_solution(16857316381816326417)
XLA Ops:
  6.5 1.8 pad_maximum_fusion
  10.3 76.0 %all-gather.3.cloned.1.call-done = bf16[768,3072]{1,0:T(8,128)(2,1)} async-done(((bf16[48,3072]{1,0:T(8,128)(2,1)}), bf16[768,3072]{1,0:T(8,128)(2,1)}) %all-gather.3.cloned.1.call-update) | async-done | bytes 4718608 | tf_op jit(solution)/shard_map/all_gather | solution.py:18
  86.3 2.0 slice-done
  88.3 3.6 %copy.48 = bf16[768,2304]{0,1:T(8,128)(2,1)} copy(bf16[768,2304]{1,0:T(8,128)(2,1)S(1)} %slice-done) | data formatting | bytes 7077888 | tf_op jit(solution)/shard_map/split | solution.py:18
  91.9 3.6 %convert_bitcast_fusion.1 = bf16[24,12,8,3,64]{4,0,2,1,3:T(8,128)(2,1)S(1)} fusion(bf16[768,3,12,64,1]{0,3,4,2,1:T(8,128)(2,1)} %bitcast.160, bf16[24,8,768,1,1]{2,1,0,4,3:T(8,128)(2,1)} %fusion.25), kind=kOutput, calls=%fused_computation.30 | convolution fusion | flops 679919616 | bytes 4718592 | tf_op jit(solution)/shard_map/rcd,dthe->rhcte/dot_general | solution.py:103
  95.5 1.5 copy.50
  97.0 2.5 reshape.90
  99.6 18.1 %all-to-all-start = ((bf16[32,9,8,192]{3,2,1,0:T(8,128)(2,1)}), bf16[32,9,8,192]{3,2,1,0:T(8,128)(2,1)S(1)}, u32[]{:S(2)}, u32[]{:S(2)}) async-start(bf16[32,9,8,192]{3,2,1,0:T(8,128)(2,1)} %reshape.90), calls=%async_computation | async-start | bytes 2359296 | tf_op jit(solution)/shard_map/all_to_all | solution.py:24
  118.5 35.5 %all-to-all-done = bf16[32,9,8,192]{3,2,1,0:T(8,128)(2,1)S(1)} async-done(((bf16[32,9,8,192]{3,2,1,0:T(8,128)(2,1)}), bf16[32,9,8,192]{3,2,1,0:T(8,128)(2,1)S(1)}, u32[]{:S(2)}, u32[]{:S(2)}) %all-to-all-start) | async-done | bytes 884768 | tf_op jit(solution)/shard_map/all_to_all | solution.py:24
  154.9 2.9 %copy.52 = bf16[9,1,256,3,64]{2,4,3,1,0:T(8,128)(2,1)S(1)} copy(bf16[9,1,256,3,64]{4,3,2,0,1:T(4,128)(2,1)S(1)} %reshape.91) | data formatting | bytes 1769472 | tf_op jit(solution)/shard_map/while | solution.py:97
  157.8 4.7 %while.20 = (s32[]{:T(128)}, bf16[9,1,256,64]{2,3,1,0:T(8,128)(2,1)S(1)}, bf16[9,1,256,3,64]{2,4,3,1,0:T(8,128)(2,1)S(1)}, s32[]{:T(128)}) while((s32[]{:T(128)}, bf16[9,1,256,64]{2,3,1,0:T(8,128)(2,1)S(1)}, bf16[9,1,256,3,64]{2,4,3,1,0:T(8,128)(2,1)S(1)}, s32[]{:T(128)}) %tuple.51), condition=%wide.region_4.5_spmd, body=%wide.region_1.4_spmd.sunk | while | flops 17251840 | bytes 1119301 | solution.py:97
  163.3 4.0 %all_to_all.55 = bf16[2,2,36864]{2,1,0:T(2,128)(2,1)S(1)} all-to-all(bf16[2,2,36864]{2,1,0:T(2,128)(2,1)S(1)} %reshape.108), channel_id=1, replica_groups=mesh['lat'=16,'lon_0'=4,'lon_1'=4,'lon_2'=2] {'lon_2'}, dimensions={0} | all-to-all | bytes 589824 | tf_op jit(solution)/shard_map/all_to_all | solution.py:53
  168.8 4.4 %all-to-all-start.2 = ((bf16[16,2,4608]{2,1,0:T(2,128)(2,1)}), bf16[16,2,4608]{2,1,0:T(2,128)(2,1)}, u32[]{:S(2)}, u32[]{:S(2)}) async-start(bf16[16,2,4608]{2,1,0:T(2,128)(2,1)} %reshape.110), calls=%async_computation.2 | async-start | bytes 589824 | tf_op jit(solution)/shard_map/all_to_all | solution.py:53
  173.2 31.5 %all-gather.5.cloned.1.call-done = bf16[768,3072]{1,0:T(8,128)(2,1)} async-done(((bf16[48,3072]{1,0:T(8,128)(2,1)}), bf16[768,3072]{1,0:T(8,128)(2,1)}) %all-gather.5.cloned.1.call-update) | async-done | bytes 4718608 | tf_op jit(solution)/shard_map/all_gather | solution.py:18
  204.7 2.0 slice-done.2
  206.7 3.6 %copy.56 = bf16[768,2304]{0,1:T(8,128)(2,1)} copy(bf16[768,2304]{1,0:T(8,128)(2,1)S(1)} %slice-done.2) | data formatting | bytes 7077888 | tf_op jit(solution)/shard_map/split | solution.py:18
  214.0 1.6 convert_bitcast_fusion
  215.7 2.4 copy.58
  218.1 2.5 reshape.96
  220.6 3.7 %all-to-all-start.3 = ((bf16[16,6,24,192]{3,2,1,0:T(8,128)(2,1)}), bf16[16,6,24,192]{3,2,1,0:T(8,128)(2,1)S(1)}, u32[]{:S(2)}, u32[]{:S(2)}) async-start(bf16[16,6,24,192]{3,2,1,0:T(8,128)(2,1)} %reshape.96), calls=%async_computation.3 | async-start | bytes 2359296 | tf_op jit(solution)/shard_map/all_to_all | solution.py:138
  224.3 27.3 %all-to-all-done.3 = bf16[16,6,24,192]{3,2,1,0:T(8,128)(2,1)S(1)} async-done(((bf16[16,6,24,192]{3,2,1,0:T(8,128)(2,1)}), bf16[16,6,24,192]{3,2,1,0:T(8,128)(2,1)S(1)}, u32[]{:S(2)}, u32[]{:S(2)}) %all-to-all-start.3) | async-done | bytes 884768 | tf_op jit(solution)/shard_map/all_to_all | solution.py:138
  253.9 4.0 %while.21 = (s32[]{:T(128)}, bf16[3,2,384,64]{2,3,1,0:T(8,128)(2,1)S(1)}, bf16[3,2,384,3,64]{2,4,1,3,0:T(8,128)(2,1)S(1)}, s32[]{:T(128)}) while((s32[]{:T(128)}, bf16[3,2,384,64]{2,3,1,0:T(8,128)(2,1)S(1)}, bf16[3,2,384,3,64]{2,4,1,3,0:T(8,128)(2,1)S(1)}, s32[]{:T(128)}) %tuple.52), condition=%wide.region_9.10_spmd, body=%wide.region_6.9_spmd.sunk | while | flops 115361280 | bytes 1185861 | solution.py:97
  259.7 8.3 %all-to-all-start.4 = ((bf16[16,2,4608]{2,1,0:T(2,128)(2,1)}), bf16[16,2,4608]{2,1,0:T(2,128)(2,1)S(1)}, u32[]{:S(2)}, u32[]{:S(2)}) async-start(bf16[16,2,4608]{2,1,0:T(2,128)(2,1)} %reshape.112), calls=%async_computation.4 | async-start | bytes 589824 | tf_op jit(solution)/shard_map/all_to_all | solution.py:140
  268.0 8.5 %all-to-all-done.4 = bf16[16,2,4608]{2,1,0:T(2,128)(2,1)S(1)} async-done(((bf16[16,2,4608]{2,1,0:T(2,128)(2,1)}), bf16[16,2,4608]{2,1,0:T(2,128)(2,1)S(1)}, u32[]{:S(2)}, u32[]{:S(2)}) %all-to-all-start.4) | async-done | bytes 294944 | tf_op jit(solution)/shard_map/all_to_all | solution.py:140
  (105 shorter events, 25.2 us)
Async XLA Ops:
  6.5 2.9 %copy-start.1 = (bf16[24,8,768]{2,1,0:T(8,128)(2,1)S(1)}, bf16[24,8,768]{2,1,0:T(8,128)(2,1)}, u32[]{:S(2)}) copy-start(bf16[24,8,768]{2,1,0:T(8,128)(2,1)} %param.11) | copy-start | bytes 884740
  6.5 2.9 %copy-start.9 = (f32[768]{0:T(1024)S(1)}, f32[768]{0:T(1024)}, u32[]{:S(2)}) copy-start(f32[768]{0:T(1024)} %param.12) | copy-start | bytes 9220
  6.5 79.8 %all-gather.3.cloned.1.call-start = ((), (), s32[]{:S(2)}) async-start(), calls=%async_computation.5 | async-start | bytes 5013504 | tf_op jit(solution)/shard_map/all_gather | solution.py:18
  86.3 2.0 slice-start
  99.5 18.2 %copy-start.7 = (bf16[48,2304]{1,0:T(8,128)(2,1)S(1)}, bf16[48,2304]{1,0:T(8,128)(2,1)}, u32[]{:S(2)}) copy-start(bf16[48,2304]{1,0:T(8,128)(2,1)} %param.16) | copy-start | bytes 663556
  99.6 18.2 %copy-start.8 = (bf16[48,768]{1,0:T(8,128)(2,1)S(1)}, bf16[48,768]{1,0:T(8,128)(2,1)}, u32[]{:S(2)}) copy-start(bf16[48,768]{1,0:T(8,128)(2,1)} %param.17) | copy-start | bytes 221188
  99.6 54.5 %all-to-all-start = ((bf16[32,9,8,192]{3,2,1,0:T(8,128)(2,1)}), bf16[32,9,8,192]{3,2,1,0:T(8,128)(2,1)S(1)}, u32[]{:S(2)}, u32[]{:S(2)}) async-start(bf16[32,9,8,192]{3,2,1,0:T(8,128)(2,1)} %reshape.90), calls=%async_computation | async-start | bytes 2359296 | tf_op jit(solution)/shard_map/all_to_all | solution.py:24
  117.7 87.0 %all-gather.5.cloned.1.call-start = ((), (), s32[]{:S(2)}) async-start(), calls=%async_computation.6 | async-start | bytes 5013504 | tf_op jit(solution)/shard_map/all_gather | solution.py:18
  154.9 2.9 %copy-start.5 = (bf16[9,1,256,64]{2,3,1,0:T(8,128)(2,1)S(1)}, bf16[9,1,256,64]{2,3,1,0:T(8,128)(2,1)}, u32[]{:S(2)}) copy-start(bf16[9,1,256,64]{2,3,1,0:T(8,128)(2,1)} %custom-call) | copy-start | bytes 884740
  168.8 41.4 %all-to-all-start.2 = ((bf16[16,2,4608]{2,1,0:T(2,128)(2,1)}), bf16[16,2,4608]{2,1,0:T(2,128)(2,1)}, u32[]{:S(2)}, u32[]{:S(2)}) async-start(bf16[16,2,4608]{2,1,0:T(2,128)(2,1)} %reshape.110), calls=%async_computation.2 | async-start | bytes 589824 | tf_op jit(solution)/shard_map/all_to_all | solution.py:53
  204.7 2.0 slice-start.2
  210.3 1.5 slice-start.1
  210.3 1.5 copy-start.2
  211.8 0.7 copy-start.10
  211.8 2.2 copy-start
  212.4 0.8 copy-start.3
  220.6 31.1 %all-to-all-start.3 = ((bf16[16,6,24,192]{3,2,1,0:T(8,128)(2,1)}), bf16[16,6,24,192]{3,2,1,0:T(8,128)(2,1)S(1)}, u32[]{:S(2)}, u32[]{:S(2)}) async-start(bf16[16,6,24,192]{3,2,1,0:T(8,128)(2,1)} %reshape.96), calls=%async_computation.3 | async-start | bytes 2359296 | tf_op jit(solution)/shard_map/all_to_all | solution.py:138
  252.4 1.5 copy-start.6
  259.7 16.8 %all-to-all-start.4 = ((bf16[16,2,4608]{2,1,0:T(2,128)(2,1)}), bf16[16,2,4608]{2,1,0:T(2,128)(2,1)S(1)}, u32[]{:S(2)}, u32[]{:S(2)}) async-start(bf16[16,2,4608]{2,1,0:T(2,128)(2,1)} %reshape.112), calls=%async_computation.4 | async-start | bytes 589824 | tf_op jit(solution)/shard_map/all_to_all | solution.py:140
  277.0 1.3 slice-start.3
  277.0 1.4 copy-start.4
Sparse Core Ops, SparseCore 0:
  9.4 76.8 all-gather.2
  120.6 84.0 all-gather.4
where the time goes:
time: 289 us; the launch traced here: 286 us
  waiting for transfers between devices  179 us (62%)
  local copies, waits for them, and re-layouts  35.3 us (12%)
  starting transfers between devices  34.5 us (12%)
  matrix products  14.6 us (5%)
  between operations  13.8 us (5%)
  other arithmetic  5.23 us (2%)
  blocking collectives  3.98 us (1%)
    all_gather x2, waiting for transfers between devices, side_by_side(): lax.all_gather(both, axis, axis=dim, tiled=True)  107 us
    all_to_all x1, waiting for transfers between devices, moved(): lax.all_to_all(group, axis, split_axis=split_dim, concat_axis=concat_dim,...  35.5 us
    all_to_all x1, waiting for transfers between devices, body(): lax.all_to_all(merid_packed, 'lat', split_axis=0, concat_axis=2, tiled=True)  27.3 us
    all_to_all x1, starting transfers between devices, moved(): lax.all_to_all(group, axis, split_axis=split_dim, concat_axis=concat_dim,...  18.1 us
    split x10, local copies, waits for them, and re-layouts, side_by_side(): jnp.split(lax.all_gather(both, axis, axis=dim, tiled=True), ends, axis=al...  12.3 us
    all_to_all x1, waiting for transfers between devices, body(): lax.all_to_all(merid_mixed, 'lat', split_axis=2, concat_axis=0, tiled=True)  8.51 us
    all_to_all x1, starting transfers between devices, body(): lax.all_to_all(merid_mixed, 'lat', split_axis=2, concat_axis=0, tiled=True)  8.31 us
    unnamed x29, local copies, waits for them, and re-layouts  6.87 us
  transfers between devices with their start and end apart: 6, of which 5 were waited for; matrix products, arithmetic and copies ran while one was open for 6% of the time, Pallas kernels for 0%

commit v1 on v0

v1 whole, which is shorter than its diff:
```python
import functools

import jax
import jax.numpy as jnp
from jax import lax
from jax.experimental import pallas as pl
from jax.experimental.pallas import tpu as pltpu
from jax.sharding import PartitionSpec as P

MESH = pl.DeviceIdType.MESH
F32 = jnp.float32
BF16 = jnp.bfloat16
EPS = 1e-05
NX, NG, NZ, NY = 4, 8, 8, 2


def norm(values, gain):
    factor = lax.rsqrt(jnp.mean(values * values, axis=-1, keepdims=True) + EPS)
    return (values * factor * gain).astype(BF16)


def matmul(a, b):
    return jnp.dot(a, b, preferred_element_type=F32)


def weights_of(query, keys):
    scores = lax.dot_general(query, keys, (((1,), (1,)), ((), ())), preferred_element_type=F32) * 0.125
    powers = jnp.exp(scores - jnp.max(scores, axis=-1, keepdims=True))
    return (powers * (1.0 / jnp.sum(powers, axis=-1, keepdims=True))).astype(BF16)


def kernel(
    tok, gz, wz_in, oz_in, gm, wm_in, om_in, out,
    wz_s, wm_s, wz, oz, wm, om, t_buf, h_buf, s_buf, u_buf, h2_buf, mz, mm, after,
    w_sem, a_sem, b_sem, c_sem, d_sem, send,
):
    lat, lon = lax.axis_index("lat"), lax.axis_index("lon")
    yl, z = lat // NZ, lax.rem(lat, NZ)
    x, g = lon // NG, lax.rem(lon, NG)
    yh, c = g // 2, lax.rem(g, 2)
    sibling = lon + 1 - 2 * c
    pair = (1 - yl) * NZ + z

    def remote(src, dst, ssem, rsem, to_lat, to_lon):
        return pltpu.make_async_remote_copy(
            src_ref=src, dst_ref=dst, send_sem=ssem, recv_sem=rsem,
            device_id=(to_lat, to_lon), device_id_type=MESH,
        )

    def local(src, dst, sem):
        return pltpu.make_async_copy(src, dst, sem)

    barrier = pltpu.get_barrier_semaphore()

    @pl.loop(1, NX * NG)
    def _(k):
        pl.semaphore_signal(barrier, inc=1, device_id=(lat, lax.rem(lon + k, NX * NG)), device_id_type=MESH)

    @pl.loop(1, NY * NZ)
    def _(k):
        pl.semaphore_signal(barrier, inc=1, device_id=(lax.rem(lat + k, NY * NZ), lon), device_id_type=MESH)

    for i in range(NX):
        @pl.when(x == i)
        def _():
            rows = wz_in[...].astype(F32)
            def part(t, low, high):
                return rows[:, 768 * t + 192 * i + low : 768 * t + 192 * i + high]
            wz_s[:, 0:128] = part(0, 0, 128).astype(BF16)
            wz_s[:, 128:256] = part(1, 0, 128).astype(BF16)
            wz_s[:, 256:384] = part(2, 0, 128).astype(BF16)
            wz_s[:, 384:512] = jnp.concatenate([part(2, 128, 192), part(0, 128, 192)], axis=1).astype(BF16)
            wz_s[:, 512:640] = jnp.concatenate([jnp.zeros((48, 64), F32), part(1, 128, 192)], axis=1).astype(BF16)
    for h in range(2):
        for t in range(3):
            wm_s[h, :, 384 * t : 384 * t + 384] = wm_in[:, 768 * t + 384 * h : 768 * t + 384 * h + 384]

    pl.semaphore_wait(barrier, NX * NG - 1 + NY * NZ - 1)

    near = [(0, 1), (2, 0), (2, 1), (1, 0), (3, 0), (1, 1), (3, 1)]

    def place(dy, dc):
        return lax.rem(yh + dy, 4) * 2 + lax.rem(c + dc, 2)

    own_rows = pl.ds(3 * g, 3)
    local(tok.at[own_rows], t_buf.at[x, g], a_sem.at[lon]).start()
    for dy, dc in near:
        to = place(dy, dc)
        remote(tok.at[pl.ds(3 * to, 3)], t_buf.at[x, g], send.at[0], a_sem.at[lon], lat, x * NG + to).start()

    emits_z = lax.rem(z, 2) == c

    @pl.when(emits_z)
    def _():
        local(wz_s, wz.at[pl.ds(48 * lat, 48)], w_sem.at[0, lat]).start()

        @pl.loop(1, NY * NZ)
        def _(k):
            remote(wz_s, wz.at[pl.ds(48 * lat, 48)], send.at[1], w_sem.at[0, lat], lax.rem(lat + k, NY * NZ), lon).start()

    def onward(source, src):
        for dx in (1, 3, 2):
            remote(src, t_buf.at[x, source], send.at[2], a_sem.at[x * NG + source], lat, lax.rem(x + dx, NX) * NG + g).start()

    onward(g, tok.at[own_rows])
    for dy, dc in [(0, 1), (1, 0), (3, 0), (1, 1), (3, 1), (2, 0), (2, 1)]:
        source = place(dy, dc)
        local(t_buf.at[x, source], t_buf.at[x, source], a_sem.at[x * NG + source]).wait()
        onward(source, t_buf.at[x, source])

    @pl.loop(0, NZ)
    def _(k):
        source = (k // 4) * NZ + 2 * lax.rem(k, 4) + c
        block = wz.at[pl.ds(48 * source, 48)]
        local(block, block, w_sem.at[0, source]).wait()
        remote(block, block, send.at[3], w_sem.at[0, source], lat, sibling).start()

    emits = z == 2 * x + c
    packs = ((1, oz_in, oz, 4), (2, wm_s, wm, 6), (3, om_in, om, 8))

    @pl.when(emits)
    def _():
        for p, src, dst, s in packs:
            block = dst.at[pl.ds(48 * lat, 48)]
            local(src.at[yl] if p == 2 else src, block, w_sem.at[p, lat]).start()

            @pl.loop(1, NY * NZ)
            def _(k):
                to = lax.rem(lat + k, NY * NZ)
                piece = src.at[to // NZ] if p == 2 else src
                remote(piece, block, send.at[s], w_sem.at[p, lat], to, lon).start()

    def relay(p, dst, s):
        for y in range(NY):
            source = y * NZ + 2 * x + c
            block = dst.at[pl.ds(48 * source, 48)]
            local(block, block, w_sem.at[p, source]).wait()
            for dx in (1, 3, 2):
                remote(block, block, send.at[s + 1], w_sem.at[p, source], lat, lax.rem(x + dx, NX) * NG + g).start()
            remote(block, block, send.at[s + 1], w_sem.at[p, source], lat, sibling).start()

    def share(p, dst, s):
        for dx in (1, 3, 2):
            for y in range(NY):
                source = y * NZ + 2 * lax.rem(x + dx, NX) + c
                block = dst.at[pl.ds(48 * source, 48)]
                local(block, block, w_sem.at[p, source]).wait()
                remote(block, block, send.at[s + 1], w_sem.at[p, source], lat, sibling).start()

    def settle(p, dst):
        @pl.loop(0, NZ)
        def _(k):
            source = (k // 4) * NZ + 2 * lax.rem(k, 4) + 1 - c
            block = dst.at[pl.ds(48 * source, 48)]
            local(block, block, w_sem.at[p, source]).wait()

    relay(1, oz, 4)

    for dx in (1, 3, 2):
        @pl.loop(0, NG)
        def _(k):
            place_x = lax.rem(x + dx, NX)
            block = t_buf.at[place_x, k]
            local(block, block, a_sem.at[place_x * NG + k]).wait()
    local(t_buf.at[x, g], t_buf.at[x, g], a_sem.at[lon]).wait()
    settle(0, wz)

    low256 = lax.broadcasted_iota(jnp.int32, (256, 128), 1) < 64
    zero256 = jnp.zeros((256, 128), BF16)

    @pl.loop(0, 3)
    def _(r):
        values = t_buf[:, :, r].astype(F32).reshape(256, 768)
        normed = norm(values, gz[...])
        fields = matmul(normed, wz[...]).astype(BF16)
        q, k, v = fields[:, 0:128], fields[:, 128:256], fields[:, 256:384]
        vq, pad_k = fields[:, 384:512], fields[:, 512:640]
        m0 = matmul(weights_of(q, jnp.where(low256, k, zero256)), v)
        m1 = matmul(weights_of(q, jnp.where(low256, zero256, k)), v)
        m2 = matmul(weights_of(vq, pad_k), vq)
        mz[:, pl.ds(r, 1), :, 0:128] = jnp.where(low256, m0, m1).reshape(32, 1, 8, 128).astype(BF16)
        mz[:, pl.ds(r, 1), :, 128:192] = m2[:, 0:64].reshape(32, 1, 8, 64).astype(BF16)

    local(mz.at[lon], h_buf.at[x, own_rows], b_sem.at[lon]).start()

    @pl.loop(1, NX * NG)
    def _(k):
        to = lax.rem(lon + k, NX * NG)
        remote(mz.at[to], h_buf.at[x, own_rows], send.at[10], b_sem.at[lon], lat, to).start()

    share(1, oz, 4)
    relay(2, wm, 6)
    settle(1, oz)

    @pl.loop(0, NX * NG)
    def _(k):
        block = h_buf.at[k // NG, pl.ds(3 * lax.rem(k, NG), 3)]
        local(block, block, b_sem.at[k]).wait()

    total = tok[...].astype(F32).reshape(192, 768)
    for i in range(NX):
        mixed = h_buf[i].astype(F32).reshape(192, 192).astype(BF16)
        total += matmul(mixed, oz[192 * i : 192 * i + 192, :])
    by_row = total.astype(BF16)
    ii = lax.broadcasted_iota(jnp.int32, (192, 192), 1)
    jj = lax.broadcasted_iota(jnp.int32, (192, 192), 0)
    turn = jnp.where((ii & 7) * 24 + (ii >> 3) == jj, 1.0, 0.0).astype(BF16)
    by_col = matmul(turn, by_row)
    after[...] = by_col
    s_buf[...] = by_col.reshape(8, 3, 8, 768).astype(BF16)

    local(s_buf.at[z], u_buf.at[yl, z], c_sem.at[lat]).start()
    for dz in (4, 3, 5, 2, 6, 1, 7):
        to = lax.rem(z + dz, NZ)
        remote(s_buf.at[to], u_buf.at[yl, z], send.at[11], c_sem.at[lat], yl * NZ + to, lon).start()
    remote(s_buf.at[z], u_buf.at[yl, z], send.at[12], c_sem.at[lat], pair, lon).start()
    for dz in (1, 7, 2, 6, 3, 5, 4):
        source = lax.rem(z + dz, NZ)
        block = u_buf.at[yl, source]
        local(block, block, c_sem.at[yl * NZ + source]).wait()
        remote(block, block, send.at[12], c_sem.at[yl * NZ + source], pair, lon).start()

    share(2, wm, 6)
    relay(3, om, 8)
    settle(2, wm)

    local(u_buf.at[yl, z], u_buf.at[yl, z], c_sem.at[lat]).wait()

    @pl.loop(0, NZ)
    def _(k):
        block = u_buf.at[1 - yl, k]
        local(block, block, c_sem.at[(1 - yl) * NZ + k]).wait()

    low384 = lax.broadcasted_iota(jnp.int32, (384, 128), 1) < 64
    zero384 = jnp.zeros((384, 128), BF16)
    normed = norm(u_buf[...].astype(F32).reshape(384, 768), gm[...])
    for j in range(3):
        at = 128 * j
        q = matmul(normed, wm[:, at : at + 128]).astype(BF16)
        k = matmul(normed, wm[:, 384 + at : 512 + at]).astype(BF16)
        v = matmul(normed, wm[:, 768 + at : 896 + at]).astype(BF16)
        m0 = matmul(weights_of(q, jnp.where(low384, k, zero384)), v)
        m1 = matmul(weights_of(q, jnp.where(low384, zero384, k)), v)
        mm[:, :, :, at : at + 128] = jnp.where(low384, m0, m1).reshape(16, 3, 8, 128).astype(BF16)

    local(mm.at[lat], h2_buf.at[yl, z], d_sem.at[lat]).start()

    @pl.loop(1, NY * NZ)
    def _(k):
        to = lax.rem(lat + k, NY * NZ)
        remote(mm.at[to], h2_buf.at[yl, z], send.at[13], d_sem.at[lat], to, lon).start()

    share(3, om, 8)
    settle(3, om)

    @pl.loop(0, NY * NZ)
    def _(k):
        block = h2_buf.at[k // NZ, lax.rem(k, NZ)]
        local(block, block, d_sem.at[k]).wait()

    total = after[...]
    for i in range(NY):
        mixed = h2_buf[i].astype(F32).reshape(192, 384).astype(BF16)
        total += matmul(mixed, om[384 * i : 384 * i + 384, :])
    back = jnp.where((jj & 7) * 24 + (jj >> 3) == ii, 1.0, 0.0).astype(BF16)
    out[...] = matmul(back, total.astype(BF16)).reshape(24, 8, 768).astype(BF16)

    def drain(sem, ref):
        local(ref, ref, sem).wait()

    drain(send.at[0], t_buf.at[0, pl.ds(0, NG - 1)])
    drain(send.at[2], t_buf.at[pl.ds(0, 3)])

    @pl.when(emits_z)
    def _():
        drain(send.at[1], wz.at[pl.ds(0, 720)])

    drain(send.at[3], wz.at[pl.ds(0, 384)])

    @pl.when(emits)
    def _():
        for p, src, dst, s in packs:
            drain(send.at[s], dst.at[pl.ds(0, 720)])

    for p, src, dst, s in packs:
        drain(send.at[s + 1], dst.at[pl.ds(0, 672)])
    drain(send.at[10], mz.at[pl.ds(0, NX * NG - 1)])
    drain(send.at[11], s_buf.at[pl.ds(0, NZ - 1)])
    drain(send.at[12], s_buf)
    drain(send.at[13], mm.at[pl.ds(0, NY * NZ - 1)])


def body(tokens, gain_zonal, qkv_zonal, out_zonal, gain_merid, qkv_merid, out_merid):
    return pl.pallas_call(
        kernel,
        out_shape=jax.ShapeDtypeStruct(tokens.shape, BF16),
        in_specs=[pl.BlockSpec(memory_space=pltpu.VMEM)] * 7,
        out_specs=pl.BlockSpec(memory_space=pltpu.VMEM),
        scratch_shapes=[
            pltpu.VMEM((48, 640), BF16),
            pltpu.VMEM((2, 48, 1152), BF16),
            pltpu.VMEM((768, 640), BF16),
            pltpu.VMEM((768, 768), BF16),
            pltpu.VMEM((768, 1152), BF16),
            pltpu.VMEM((768, 768), BF16),
            pltpu.VMEM((NX, NG, 3, 8, 768), BF16),
            pltpu.VMEM((NX, 24, 8, 192), BF16),
            pltpu.VMEM((8, 3, 8, 768), BF16),
            pltpu.VMEM((NY, NZ, 3, 8, 768), BF16),
            pltpu.VMEM((NY, NZ, 3, 8, 384), BF16),
            pltpu.VMEM((NX * NG, 3, 8, 192), BF16),
            pltpu.VMEM((NY * NZ, 3, 8, 384), BF16),
            pltpu.VMEM((192, 768), F32),
            pltpu.SemaphoreType.DMA((4, NY * NZ)),
            pltpu.SemaphoreType.DMA((NX * NG,)),
            pltpu.SemaphoreType.DMA((NX * NG,)),
            pltpu.SemaphoreType.DMA((NY * NZ,)),
            pltpu.SemaphoreType.DMA((NY * NZ,)),
            pltpu.SemaphoreType.DMA((14,)),
        ],
        compiler_params=pltpu.CompilerParams(
            collective_id=0, has_side_effects=True, vmem_limit_bytes=56 * 1024 * 1024
        ),
        name="axial",
    )(tokens, gain_zonal.reshape(1, -1), qkv_zonal, out_zonal, gain_merid.reshape(1, -1), qkv_merid, out_merid)


def solution(mesh):
    return jax.shard_map(
        body,
        mesh=mesh,
        in_specs=(
            P("lat", "lon", None),
            P(),
            P("lat", None),
            P("lat", None),
            P(),
            P("lat", None),
            P("lat", None),
        ),
        out_specs=P("lat", "lon", None),
        check_vma=False,
    )
```

time: 289 us -> 108 us (0.37)
  the two profiles are of different devices: /device:TPU:1 before, /device:TPU:24 now
where the time goes in v1:
time: 108 us
  Pallas kernels  104 us (96%)
  local copies, waits for them, and re-layouts  3.57 us (3%)
    pallas_call x1, Pallas kernels, body(): pl.pallas_call(kernel, out_shape=jax.ShapeDtypeStruct(tokens.shape, BF16)...  104 us

profile of v1, /device:TPU:24, one launch (start us, length us, event | category | flops | bytes accessed | tf_op | source)
XLA Modules:
  0.0 107.6 jit_solution(14813794686573831971)
XLA Ops:
  0.0 0.0 copy-start
  0.0 1.3 %reshape.6.gz = f32[1,768]{1,0:T(1,128)} reshape(f32[768]{0:T(1024)} %param.8) | data formatting | bytes 6144 | tf_op jit(solution)/shard_map/reshape | solution.py:325
  1.3 0.0 copy-done
  1.3 0.6 reshape.7.gm
  1.9 104.0 %axial.1 = bf16[24,8,768]{2,1,0:T(8,128)(2,1)} custom-call(bf16[24,8,768]{2,1,0:T(8,128)(2,1)} %tok.1, f32[1,768]{1,0:T(1,128)} %reshape.6.gz, bf16[48,2304]{1,0:T(8,128)(2,1)} %wz_in.1, bf16[48,768]{1,0:T(8,128)(2,1)} %oz_in.1, f32[1,768]{1,0:T(1,128)} %reshape.7.gm, bf16[48,2304]{1,0:T(8,128)(2,1)} %wm_in.1, bf16[48,768]{1,0:T(8,128)(2,1)} %om_in.1), custom_call_target="tpu_custom_call" | custom-call | tf_op jit(solution)/shard_map/axial/pallas_call | solution.py:294
  105.9 1.7 %copy.9 = bf16[24,8,768]{2,1,0:T(8,128)(2,1)} copy(bf16[24,8,768]{2,1,0:T(8,128)(2,1)} %axial.1) | data formatting | bytes 589824
Async XLA Ops:
  0.0 1.3 %copy-start = (f32[768]{0:T(1024)S(1)}, f32[768]{0:T(1024)}, u32[]{:S(2)}) copy-start(f32[768]{0:T(1024)} %param.11) | copy-start | bytes 9220

commit v2 on v1

--- a/solution.py
+++ b/solution.py
@@ -49,6 +49,9 @@
 
     def local(src, dst, sem):
         return pltpu.make_async_copy(src, dst, sem)
+
+    def wait(ref, sem):
+        local(ref, ref, sem).wait()
 
     barrier = pltpu.get_barrier_semaphore()
 
@@ -77,101 +80,160 @@
 
     pl.semaphore_wait(barrier, NX * NG - 1 + NY * NZ - 1)
 
-    near = [(0, 1), (2, 0), (2, 1), (1, 0), (3, 0), (1, 1), (3, 1)]
-
     def place(dy, dc):
         return lax.rem(yh + dy, 4) * 2 + lax.rem(c + dc, 2)
 
     own_rows = pl.ds(3 * g, 3)
     local(tok.at[own_rows], t_buf.at[x, g], a_sem.at[lon]).start()
-    for dy, dc in near:
+    for dy, dc in [(0, 1), (2, 0), (2, 1), (1, 0), (3, 0), (1, 1), (3, 1)]:
         to = place(dy, dc)
         remote(tok.at[pl.ds(3 * to, 3)], t_buf.at[x, g], send.at[0], a_sem.at[lon], lat, x * NG + to).start()
-
-    emits_z = lax.rem(z, 2) == c
-
-    @pl.when(emits_z)
-    def _():
-        local(wz_s, wz.at[pl.ds(48 * lat, 48)], w_sem.at[0, lat]).start()
-
-        @pl.loop(1, NY * NZ)
-        def _(k):
-            remote(wz_s, wz.at[pl.ds(48 * lat, 48)], send.at[1], w_sem.at[0, lat], lax.rem(lat + k, NY * NZ), lon).start()
 
     def onward(source, src):
         for dx in (1, 3, 2):
             remote(src, t_buf.at[x, source], send.at[2], a_sem.at[x * NG + source], lat, lax.rem(x + dx, NX) * NG + g).start()
 
     onward(g, tok.at[own_rows])
-    for dy, dc in [(0, 1), (1, 0), (3, 0), (1, 1), (3, 1), (2, 0), (2, 1)]:
-        source = place(dy, dc)
-        local(t_buf.at[x, source], t_buf.at[x, source], a_sem.at[x * NG + source]).wait()
-        onward(source, t_buf.at[x, source])
-
-    @pl.loop(0, NZ)
-    def _(k):
-        source = (k // 4) * NZ + 2 * lax.rem(k, 4) + c
-        block = wz.at[pl.ds(48 * source, 48)]
-        local(block, block, w_sem.at[0, source]).wait()
-        remote(block, block, send.at[3], w_sem.at[0, source], lat, sibling).start()
-
-    emits = z == 2 * x + c
+
+    def rows_of(dst, source):
+        return dst.at[pl.ds(48 * source, 48)]
+
+    def along(p, dst, s, source, src, steps):
+        for dz in steps:
+            remote(src, rows_of(dst, source), send.at[s], w_sem.at[p, source], yl * NZ + lax.rem(z + dz, NZ), lon).start()
+
+    def emit(p, src, dst, s):
+        mine, theirs = (src.at[yl], src.at[1 - yl]) if p == 2 else (src, src)
+        remote(theirs, rows_of(dst, lat), send.at[s], w_sem.at[p, lat], pair, lon).start()
+        local(mine, rows_of(dst, lat), w_sem.at[p, lat]).start()
+        along(p, dst, s, lat, mine, (1, 7, 2, 6))
+
+    active = lax.rem(z, 2) == c
+
+    @pl.when(active)
+    def _():
+        emit(0, wz_s, wz, 1)
+
+    dz_own = lax.rem(z + NZ - 2 * x - c, NZ)
+    source_own, source_far = yl * NZ + 2 * x + c, (1 - yl) * NZ + 2 * x + c
     packs = ((1, oz_in, oz, 4), (2, wm_s, wm, 6), (3, om_in, om, 8))
 
-    @pl.when(emits)
-    def _():
-        for p, src, dst, s in packs:
-            block = dst.at[pl.ds(48 * lat, 48)]
-            local(src.at[yl] if p == 2 else src, block, w_sem.at[p, lat]).start()
-
-            @pl.loop(1, NY * NZ)
-            def _(k):
-                to = lax.rem(lat + k, NY * NZ)
-                piece = src.at[to // NZ] if p == 2 else src
-                remote(piece, block, send.at[s], w_sem.at[p, lat], to, lon).start()
-
-    def relay(p, dst, s):
-        for y in range(NY):
-            source = y * NZ + 2 * x + c
-            block = dst.at[pl.ds(48 * source, 48)]
-            local(block, block, w_sem.at[p, source]).wait()
+    def first(p, src, dst, s):
+        @pl.when(dz_own == 0)
+        def _():
+            emit(p, src, dst, s)
+
+    def second(p, src, dst, s):
+        @pl.when(dz_own == 0)
+        def _():
+            wait(rows_of(dst, source_own), w_sem.at[p, source_own])
+            wait(rows_of(dst, source_far), w_sem.at[p, source_far])
+            along(p, dst, s, source_far, rows_of(dst, source_far), (1, 7, 2, 6))
+
+    def third(p, src, dst, s):
+        for at, steps in ((2, (1, 2)), (6, (7,))):
+            @pl.when(dz_own == at)
+            def _():
+                for source in (source_own, source_far):
+                    wait(rows_of(dst, source), w_sem.at[p, source])
+                    along(p, dst, s, source, rows_of(dst, source), steps)
+
+    def relay(p, src, dst, s):
+        for source in (source_own, source_far):
+            block = rows_of(dst, source)
+
+            @pl.when((dz_own != 0) & (dz_own != 2) & (dz_own != 6))
+            def _():
+                wait(block, w_sem.at[p, source])
+
             for dx in (1, 3, 2):
                 remote(block, block, send.at[s + 1], w_sem.at[p, source], lat, lax.rem(x + dx, NX) * NG + g).start()
             remote(block, block, send.at[s + 1], w_sem.at[p, source], lat, sibling).start()
 
-    def share(p, dst, s):
+    def share(p, src, dst, s):
         for dx in (1, 3, 2):
             for y in range(NY):
                 source = y * NZ + 2 * lax.rem(x + dx, NX) + c
-                block = dst.at[pl.ds(48 * source, 48)]
-                local(block, block, w_sem.at[p, source]).wait()
+                block = rows_of(dst, source)
+                wait(block, w_sem.at[p, source])
                 remote(block, block, send.at[s + 1], w_sem.at[p, source], lat, sibling).start()
 
     def settle(p, dst):
         @pl.loop(0, NZ)
         def _(k):
             source = (k // 4) * NZ + 2 * lax.rem(k, 4) + 1 - c
-            block = dst.at[pl.ds(48 * source, 48)]
-            local(block, block, w_sem.at[p, source]).wait()
-
-    relay(1, oz, 4)
+            wait(rows_of(dst, source), w_sem.at[p, source])
+
+    first(*packs[0])
+
+    def pass_on(pieces):
+        for dy, dc in pieces:
+            source = place(dy, dc)
+            wait(t_buf.at[x, source], a_sem.at[x * NG + source])
+            onward(source, t_buf.at[x, source])
+
+    pass_on([(0, 1)])
+
+    @pl.when(active)
+    def _():
+        wait(rows_of(wz, pair), w_sem.at[0, pair])
+        along(0, wz, 1, pair, rows_of(wz, pair), (1, 7, 2, 6))
+
+    second(*packs[0])
+    pass_on([(1, 0), (3, 0), (1, 1), (3, 1)])
+
+    def to_sibling(source):
+        block = rows_of(wz, source)
+        remote(block, block, send.at[3], w_sem.at[0, source], lat, sibling).start()
+
+    @pl.when(active)
+    def _():
+        for y in (yl, 1 - yl):
+            for dz, steps in ((6, (1, 2)), (2, (7,))):
+                source = y * NZ + lax.rem(z + dz, NZ)
+                wait(rows_of(wz, source), w_sem.at[0, source])
+                along(0, wz, 1, source, rows_of(wz, source), steps)
+                to_sibling(source)
+
+    third(*packs[0])
+    first(*packs[1])
+    pass_on([(2, 0), (2, 1)])
+
+    @pl.when(active)
+    def _():
+        wait(rows_of(wz, lat), w_sem.at[0, lat])
+        to_sibling(lat)
+        to_sibling(pair)
+        for y in (yl, 1 - yl):
+            source = y * NZ + lax.rem(z + 4, NZ)
+            wait(rows_of(wz, source), w_sem.at[0, source])
+            to_sibling(source)
+
+    @pl.when(jnp.logical_not(active))
+    def _():
+        for y in (yl, 1 - yl):
+            for dz in (1, 7, 3, 5):
+                source = y * NZ + lax.rem(z + dz, NZ)
+                wait(rows_of(wz, source), w_sem.at[0, source])
+                to_sibling(source)
+
+    second(*packs[1])
 
     for dx in (1, 3, 2):
         @pl.loop(0, NG)
         def _(k):
             place_x = lax.rem(x + dx, NX)
-            block = t_buf.at[place_x, k]
-            local(block, block, a_sem.at[place_x * NG + k]).wait()
-    local(t_buf.at[x, g], t_buf.at[x, g], a_sem.at[lon]).wait()
+            wait(t_buf.at[place_x, k], a_sem.at[place_x * NG + k])
+    wait(t_buf.at[x, g], a_sem.at[lon])
+    relay(*packs[0])
     settle(0, wz)
 
     low256 = lax.broadcasted_iota(jnp.int32, (256, 128), 1) < 64
     zero256 = jnp.zeros((256, 128), BF16)
 
-    @pl.loop(0, 3)
-    def _(r):
+    def zonal_row(r):
         values = t_buf[:, :, r].astype(F32).reshape(256, 768)
-        normed = norm(values, gz[...])
+        normed = norm(values, gz[...].reshape(1, 768))
         fields = matmul(normed, wz[...]).astype(BF16)
         q, k, v = fields[:, 0:128], fields[:, 128:256], fields[:, 256:384]
         vq, pad_k = fields[:, 384:512], fields[:, 512:640]
@@ -181,21 +243,34 @@
         mz[:, pl.ds(r, 1), :, 0:128] = jnp.where(low256, m0, m1).reshape(32, 1, 8, 128).astype(BF16)
         mz[:, pl.ds(r, 1), :, 128:192] = m2[:, 0:64].reshape(32, 1, 8, 64).astype(BF16)
 
-    local(mz.at[lon], h_buf.at[x, own_rows], b_sem.at[lon]).start()
-
-    @pl.loop(1, NX * NG)
-    def _(k):
-        to = lax.rem(lon + k, NX * NG)
-        remote(mz.at[to], h_buf.at[x, own_rows], send.at[10], b_sem.at[lon], lat, to).start()
-
-    share(1, oz, 4)
-    relay(2, wm, 6)
+    def home(low, rows):
+        here, there = pl.ds(low, rows), pl.ds(3 * g + low, rows)
+        local(mz.at[lon, here], h_buf.at[x, there], b_sem.at[lon]).start()
+
+        @pl.loop(1, NX * NG)
+        def _(k):
+            to = lax.rem(lon + k, NX * NG)
+            remote(mz.at[to, here], h_buf.at[x, there], send.at[10], b_sem.at[lon], lat, to).start()
+
+    zonal_row(0)
+    home(0, 1)
+
+    @pl.loop(1, 3)
+    def _(r):
+        zonal_row(r)
+
+    home(1, 2)
+
+    third(*packs[1])
+    first(*packs[2])
+    share(*packs[0])
     settle(1, oz)
+    second(*packs[2])
+    relay(*packs[1])
 
     @pl.loop(0, NX * NG)
     def _(k):
-        block = h_buf.at[k // NG, pl.ds(3 * lax.rem(k, NG), 3)]
-        local(block, block, b_sem.at[k]).wait()
+        wait(h_buf.at[k // NG, pl.ds(3 * lax.rem(k, NG), 3)], b_sem.at[k])
 
     total = tok[...].astype(F32).reshape(192, 768)
     for i in range(NX):
@@ -214,26 +289,26 @@
         to = lax.rem(z + dz, NZ)
         remote(s_buf.at[to], u_buf.at[yl, z], send.at[11], c_sem.at[lat], yl * NZ + to, lon).start()
     remote(s_buf.at[z], u_buf.at[yl, z], send.at[12], c_sem.at[lat], pair, lon).start()
+    third(*packs[2])
     for dz in (1, 7, 2, 6, 3, 5, 4):
         source = lax.rem(z + dz, NZ)
         block = u_buf.at[yl, source]
-        local(block, block, c_sem.at[yl * NZ + source]).wait()
+        wait(block, c_sem.at[yl * NZ + source])
         remote(block, block, send.at[12], c_sem.at[yl * NZ + source], pair, lon).start()
 
-    share(2, wm, 6)
-    relay(3, om, 8)
+    share(*packs[1])
+    relay(*packs[2])
     settle(2, wm)
 
-    local(u_buf.at[yl, z], u_buf.at[yl, z], c_sem.at[lat]).wait()
+    wait(u_buf.at[yl, z], c_sem.at[lat])
 
     @pl.loop(0, NZ)
     def _(k):
-        block = u_buf.at[1 - yl, k]
-        local(block, block, c_sem.at[(1 - yl) * NZ + k]).wait()
+        wait(u_buf.at[1 - yl, k], c_sem.at[(1 - yl) * NZ + k])
 
     low384 = lax.broadcasted_iota(jnp.int32, (384, 128), 1) < 64
     zero384 = jnp.zeros((384, 128), BF16)
-    normed = norm(u_buf[...].astype(F32).reshape(384, 768), gm[...])
+    normed = norm(u_buf[...].astype(F32).reshape(384, 768), gm[...].reshape(1, 768))
     for j in range(3):
         at = 128 * j
         q = matmul(normed, wm[:, at : at + 128]).astype(BF16)
@@ -241,22 +316,22 @@
         v = matmul(normed, wm[:, 768 + at : 896 + at]).astype(BF16)
         m0 = matmul(weights_of(q, jnp.where(low384, k, zero384)), v)
         m1 = matmul(weights_of(q, jnp.where(low384, zero384, k)), v)
-        mm[:, :, :, at : at + 128] = jnp.where(low384, m0, m1).reshape(16, 3, 8, 128).astype(BF16)
-
-    local(mm.at[lat], h2_buf.at[yl, z], d_sem.at[lat]).start()
-
-    @pl.loop(1, NY * NZ)
-    def _(k):
-        to = lax.rem(lat + k, NY * NZ)
-        remote(mm.at[to], h2_buf.at[yl, z], send.at[13], d_sem.at[lat], to, lon).start()
-
-    share(3, om, 8)
+        mm[j] = jnp.where(low384, m0, m1).reshape(16, 3, 8, 128).astype(BF16)
+
+        there = h2_buf.at[yl, z, :, :, pl.ds(at, 128)]
+        local(mm.at[j, lat], there, d_sem.at[lat]).start()
+
+        @pl.loop(1, NY * NZ)
+        def _(k):
+            to = lax.rem(lat + k, NY * NZ)
+            remote(mm.at[j, to], there, send.at[13], d_sem.at[lat], to, lon).start()
+
+    share(*packs[2])
     settle(3, om)
 
     @pl.loop(0, NY * NZ)
     def _(k):
-        block = h2_buf.at[k // NZ, lax.rem(k, NZ)]
-        local(block, block, d_sem.at[k]).wait()
+        wait(h2_buf.at[k // NZ, lax.rem(k, NZ)], d_sem.at[k])
 
     total = after[...]
     for i in range(NY):
@@ -265,29 +340,25 @@
     back = jnp.where((jj & 7) * 24 + (jj >> 3) == ii, 1.0, 0.0).astype(BF16)
     out[...] = matmul(back, total.astype(BF16)).reshape(24, 8, 768).astype(BF16)
 
-    def drain(sem, ref):
-        local(ref, ref, sem).wait()
-
-    drain(send.at[0], t_buf.at[0, pl.ds(0, NG - 1)])
-    drain(send.at[2], t_buf.at[pl.ds(0, 3)])
-
-    @pl.when(emits_z)
-    def _():
-        drain(send.at[1], wz.at[pl.ds(0, 720)])
-
-    drain(send.at[3], wz.at[pl.ds(0, 384)])
-
-    @pl.when(emits)
-    def _():
-        for p, src, dst, s in packs:
-            drain(send.at[s], dst.at[pl.ds(0, 720)])
-
+    wait(t_buf.at[0, pl.ds(0, NG - 1)], send.at[0])
+    wait(t_buf.at[pl.ds(0, 3)], send.at[2])
+
+    @pl.when(active)
+    def _():
+        wait(wz.at[pl.ds(0, 48 * 15)], send.at[1])
+
+    wait(wz.at[pl.ds(0, 48 * 8)], send.at[3])
     for p, src, dst, s in packs:
-        drain(send.at[s + 1], dst.at[pl.ds(0, 672)])
-    drain(send.at[10], mz.at[pl.ds(0, NX * NG - 1)])
-    drain(send.at[11], s_buf.at[pl.ds(0, NZ - 1)])
-    drain(send.at[12], s_buf)
-    drain(send.at[13], mm.at[pl.ds(0, NY * NZ - 1)])
+        for at, count in ((0, 9), (2, 4), (6, 2)):
+            @pl.when(dz_own == at)
+            def _():
+                wait(dst.at[pl.ds(0, 48 * count)], send.at[s])
+
+        wait(dst.at[pl.ds(0, 48 * 14)], send.at[s + 1])
+    wait(mz.at[pl.ds(0, NX * NG - 1)], send.at[10])
+    wait(s_buf.at[pl.ds(0, NZ - 1)], send.at[11])
+    wait(s_buf, send.at[12])
+    wait(mm.at[:, pl.ds(0, NY * NZ - 1)], send.at[13])
 
 
 def body(tokens, gain_zonal, qkv_zonal, out_zonal, gain_merid, qkv_merid, out_merid):
@@ -309,7 +380,7 @@
             pltpu.VMEM((NY, NZ, 3, 8, 768), BF16),
             pltpu.VMEM((NY, NZ, 3, 8, 384), BF16),
             pltpu.VMEM((NX * NG, 3, 8, 192), BF16),
-            pltpu.VMEM((NY * NZ, 3, 8, 384), BF16),
+            pltpu.VMEM((3, NY * NZ, 3, 8, 128), BF16),
             pltpu.VMEM((192, 768), F32),
             pltpu.SemaphoreType.DMA((4, NY * NZ)),
             pltpu.SemaphoreType.DMA((NX * NG,)),
@@ -322,7 +393,7 @@
             collective_id=0, has_side_effects=True, vmem_limit_bytes=56 * 1024 * 1024
         ),
         name="axial",
-    )(tokens, gain_zonal.reshape(1, -1), qkv_zonal, out_zonal, gain_merid.reshape(1, -1), qkv_merid, out_merid)
+    )(tokens, gain_zonal, qkv_zonal, out_zonal, gain_merid, qkv_merid, out_merid)
 
 
 def solution(mesh):

time: 108 us -> 83.5 us (0.77)
  the two profiles are of different devices: /device:TPU:24 before, /device:TPU:1 now
where the time goes in v2:
time: 83.5 us; the launch traced here: 83.3 us
  Pallas kernels  81.6 us (98%)
  local copies, waits for them, and re-layouts  1.69 us (2%)
    pallas_call x1, Pallas kernels, body(): pl.pallas_call(kernel, out_shape=jax.ShapeDtypeStruct(tokens.shape, BF16)...  81.6 us
    unnamed x1, local copies, waits for them, and re-layouts  1.69 us

profile of v2, /device:TPU:1, one launch (start us, length us, event | category | flops | bytes accessed | tf_op | source)
XLA Modules:
  0.0 83.3 jit_solution(10626284829069342739)
XLA Ops:
  0.0 81.6 %axial.1 = bf16[24,8,768]{2,1,0:T(8,128)(2,1)} custom-call(bf16[24,8,768]{2,1,0:T(8,128)(2,1)} %tok.1, f32[768]{0:T(1024)} %gz.1, bf16[48,2304]{1,0:T(8,128)(2,1)} %wz_in.1, bf16[48,768]{1,0:T(8,128)(2,1)} %oz_in.1, f32[768]{0:T(1024)} %gm.1, bf16[48,2304]{1,0:T(8,128)(2,1)} %wm_in.1, bf16[48,768]{1,0:T(8,128)(2,1)} %om_in.1), custom_call_target="tpu_custom_call" | custom-call | tf_op jit(solution)/shard_map/axial/pallas_call | solution.py:365
  81.6 1.7 %copy.9 = bf16[24,8,768]{2,1,0:T(8,128)(2,1)} copy(bf16[24,8,768]{2,1,0:T(8,128)(2,1)} %axial.1) | data formatting | bytes 589824

commit v3 on v2

--- a/solution.py
+++ b/solution.py
@@ -1,4 +1,4 @@
-import functools
+import math
 
 import jax
 import jax.numpy as jnp
@@ -11,6 +11,7 @@
 F32 = jnp.float32
 BF16 = jnp.bfloat16
 EPS = 1e-05
+SCALE = 0.125 * math.log2(math.e)
 NX, NG, NZ, NY = 4, 8, 8, 2
 
 
@@ -23,16 +24,17 @@
     return jnp.dot(a, b, preferred_element_type=F32)
 
 
-def weights_of(query, keys):
-    scores = lax.dot_general(query, keys, (((1,), (1,)), ((), ())), preferred_element_type=F32) * 0.125
-    powers = jnp.exp(scores - jnp.max(scores, axis=-1, keepdims=True))
-    return (powers * (1.0 / jnp.sum(powers, axis=-1, keepdims=True))).astype(BF16)
+def attend(query, keys, values):
+    scores = lax.dot_general(query, keys, (((1,), (1,)), ((), ())), preferred_element_type=F32) * SCALE
+    powers = jnp.exp2(scores - jnp.max(scores, axis=-1, keepdims=True))
+    return matmul(powers.astype(BF16), values) * (1.0 / jnp.sum(powers, axis=-1, keepdims=True))
 
 
 def kernel(
-    tok, gz, wz_in, oz_in, gm, wm_in, om_in, out,
+    tok_hbm, gz_hbm, wz_hbm, oz_hbm, gm_hbm, wm_hbm, om_hbm, out,
+    tok, gz, wz_in, oz_in, gm, wm_in, om_in,
     wz_s, wm_s, wz, oz, wm, om, t_buf, h_buf, s_buf, u_buf, h2_buf, mz, mm, after,
-    w_sem, a_sem, b_sem, c_sem, d_sem, send,
+    w_sem, a_sem, b_sem, c_sem, d_sem, send, in_sem,
 ):
     lat, lon = lax.axis_index("lat"), lax.axis_index("lon")
     yl, z = lat // NZ, lax.rem(lat, NZ)
@@ -53,7 +55,15 @@
     def wait(ref, sem):
         local(ref, ref, sem).wait()
 
+    inputs = [
+        local(src, dst, in_sem.at[k])
+        for k, (src, dst) in enumerate((
+            (wz_hbm, wz_in), (tok_hbm, tok), (wm_hbm, wm_in), (oz_hbm, oz_in), (om_hbm, om_in), (gz_hbm, gz), (gm_hbm, gm),
+        ))
+    ]
     barrier = pltpu.get_barrier_semaphore()
+    for copy in inputs:
+        copy.start()
 
     @pl.loop(1, NX * NG)
     def _(k):
@@ -62,6 +72,8 @@
     @pl.loop(1, NY * NZ)
     def _(k):
         pl.semaphore_signal(barrier, inc=1, device_id=(lax.rem(lat + k, NY * NZ), lon), device_id_type=MESH)
+
+    inputs[0].wait()
 
     for i in range(NX):
         @pl.when(x == i)
@@ -74,26 +86,8 @@
             wz_s[:, 256:384] = part(2, 0, 128).astype(BF16)
             wz_s[:, 384:512] = jnp.concatenate([part(2, 128, 192), part(0, 128, 192)], axis=1).astype(BF16)
             wz_s[:, 512:640] = jnp.concatenate([jnp.zeros((48, 64), F32), part(1, 128, 192)], axis=1).astype(BF16)
-    for h in range(2):
-        for t in range(3):
-            wm_s[h, :, 384 * t : 384 * t + 384] = wm_in[:, 768 * t + 384 * h : 768 * t + 384 * h + 384]
-
+    inputs[1].wait()
     pl.semaphore_wait(barrier, NX * NG - 1 + NY * NZ - 1)
-
-    def place(dy, dc):
-        return lax.rem(yh + dy, 4) * 2 + lax.rem(c + dc, 2)
-
-    own_rows = pl.ds(3 * g, 3)
-    local(tok.at[own_rows], t_buf.at[x, g], a_sem.at[lon]).start()
-    for dy, dc in [(0, 1), (2, 0), (2, 1), (1, 0), (3, 0), (1, 1), (3, 1)]:
-        to = place(dy, dc)
-        remote(tok.at[pl.ds(3 * to, 3)], t_buf.at[x, g], send.at[0], a_sem.at[lon], lat, x * NG + to).start()
-
-    def onward(source, src):
-        for dx in (1, 3, 2):
-            remote(src, t_buf.at[x, source], send.at[2], a_sem.at[x * NG + source], lat, lax.rem(x + dx, NX) * NG + g).start()
-
-    onward(g, tok.at[own_rows])
 
     def rows_of(dst, source):
         return dst.at[pl.ds(48 * source, 48)]
@@ -113,6 +107,27 @@
     @pl.when(active)
     def _():
         emit(0, wz_s, wz, 1)
+
+    def place(dy, dc):
+        return lax.rem(yh + dy, 4) * 2 + lax.rem(c + dc, 2)
+
+    own_rows = pl.ds(3 * g, 3)
+    local(tok.at[own_rows], t_buf.at[x, g], a_sem.at[lon]).start()
+    for dy, dc in [(0, 1), (1, 0), (3, 0), (1, 1), (3, 1), (2, 0), (2, 1)]:
+        to = place(dy, dc)
+        remote(tok.at[pl.ds(3 * to, 3)], t_buf.at[x, g], send.at[0], a_sem.at[lon], lat, x * NG + to).start()
+
+    for copy in inputs[2:]:
+        copy.wait()
+    for h in range(2):
+        for t in range(3):
+            wm_s[h, :, 384 * t : 384 * t + 384] = wm_in[:, 768 * t + 384 * h : 768 * t + 384 * h + 384]
+
+    def onward(source, src, steps=(1, 3)):
+        for dx in steps:
+            remote(src, t_buf.at[x, source], send.at[2], a_sem.at[x * NG + source], lat, lax.rem(x + dx, NX) * NG + g).start()
+
+    onward(g, tok.at[own_rows])
 
     dz_own = lax.rem(z + NZ - 2 * x - c, NZ)
     source_own, source_far = yl * NZ + 2 * x + c, (1 - yl) * NZ + 2 * x + c
@@ -146,17 +161,26 @@
             def _():
                 wait(block, w_sem.at[p, source])
 
-            for dx in (1, 3, 2):
+            for dx in ((1, 3) if p == 1 else (1, 3, 2)):
                 remote(block, block, send.at[s + 1], w_sem.at[p, source], lat, lax.rem(x + dx, NX) * NG + g).start()
             remote(block, block, send.at[s + 1], w_sem.at[p, source], lat, sibling).start()
 
+    def taken(p, dst, s, dx, y):
+        source = y * NZ + 2 * lax.rem(x + dx, NX) + c
+        block = rows_of(dst, source)
+        wait(block, w_sem.at[p, source])
+        remote(block, block, send.at[s + 1], w_sem.at[p, source], lat, sibling).start()
+        return block, source
+
+    def hop(p, src, dst, s):
+        for dx, y in ((3, yl), (1, 1 - yl)):
+            block, source = taken(p, dst, s, dx, y)
+            remote(block, block, send.at[s + 1], w_sem.at[p, source], lat, lax.rem(x + NX - dx, NX) * NG + g).start()
+
     def share(p, src, dst, s):
-        for dx in (1, 3, 2):
-            for y in range(NY):
-                source = y * NZ + 2 * lax.rem(x + dx, NX) + c
-                block = rows_of(dst, source)
-                wait(block, w_sem.at[p, source])
-                remote(block, block, send.at[s + 1], w_sem.at[p, source], lat, sibling).start()
+        rest = ((3, 1 - yl), (1, yl), (2, yl), (2, 1 - yl))
+        for dx, y in (rest if p == 1 else ((3, yl), (1, 1 - yl)) + rest):
+            taken(p, dst, s, dx, y)
 
     def settle(p, dst):
         @pl.loop(0, NZ)
@@ -170,34 +194,46 @@
         for dy, dc in pieces:
             source = place(dy, dc)
             wait(t_buf.at[x, source], a_sem.at[x * NG + source])
-            onward(source, t_buf.at[x, source])
-
-    pass_on([(0, 1)])
-
-    @pl.when(active)
-    def _():
-        wait(rows_of(wz, pair), w_sem.at[0, pair])
-        along(0, wz, 1, pair, rows_of(wz, pair), (1, 7, 2, 6))
-
-    second(*packs[0])
-    pass_on([(1, 0), (3, 0), (1, 1), (3, 1)])
+            onward(source, t_buf.at[x, source], (1, 3, 2) if dy == 2 else (1, 3))
 
     def to_sibling(source):
         block = rows_of(wz, source)
         remote(block, block, send.at[3], w_sem.at[0, source], lat, sibling).start()
 
-    @pl.when(active)
-    def _():
-        for y in (yl, 1 - yl):
+    def pass_zonal(y):
+        @pl.when(active)
+        def _():
             for dz, steps in ((6, (1, 2)), (2, (7,))):
                 source = y * NZ + lax.rem(z + dz, NZ)
                 wait(rows_of(wz, source), w_sem.at[0, source])
                 along(0, wz, 1, source, rows_of(wz, source), steps)
                 to_sibling(source)
 
+    def cross(dys):
+        for dy in dys:
+            for dx, dc in ((3, 0), (1, 1)):
+                source, from_x = place(dy, dc), lax.rem(x + dx, NX)
+                block = t_buf.at[from_x, source]
+                wait(block, a_sem.at[from_x * NG + source])
+                remote(block, block, send.at[2], a_sem.at[from_x * NG + source], lat, lax.rem(x + NX - dx, NX) * NG + g).start()
+
+    pass_on([(0, 1)])
+
+    @pl.when(active)
+    def _():
+        wait(rows_of(wz, pair), w_sem.at[0, pair])
+        along(0, wz, 1, pair, rows_of(wz, pair), (1, 7, 2, 6))
+
+    second(*packs[0])
+    pass_zonal(yl)
+    pass_on([(1, 0), (3, 0)])
+    cross([0])
+    pass_zonal(1 - yl)
+    pass_on([(1, 1), (3, 1)])
     third(*packs[0])
     first(*packs[1])
     pass_on([(2, 0), (2, 1)])
+    cross([1, 3])
 
     @pl.when(active)
     def _():
@@ -217,15 +253,21 @@
                 wait(rows_of(wz, source), w_sem.at[0, source])
                 to_sibling(source)
 
+    relay(*packs[0])
+    def arrived(dx, source):
+        from_x = lax.rem(x + dx, NX)
+        wait(t_buf.at[from_x, source], a_sem.at[from_x * NG + source])
+
+    for dy in (0, 1, 3, 2):
+        arrived(3, place(dy, 1))
+        arrived(1, place(dy, 0))
+        if dy == 2:
+            arrived(3, place(dy, 0))
+            arrived(1, place(dy, 1))
+        for dc in (0, 1):
+            arrived(2, place(dy, dc))
+    wait(t_buf.at[x, g], a_sem.at[lon])
     second(*packs[1])
-
-    for dx in (1, 3, 2):
-        @pl.loop(0, NG)
-        def _(k):
-            place_x = lax.rem(x + dx, NX)
-            wait(t_buf.at[place_x, k], a_sem.at[place_x * NG + k])
-    wait(t_buf.at[x, g], a_sem.at[lon])
-    relay(*packs[0])
     settle(0, wz)
 
     low256 = lax.broadcasted_iota(jnp.int32, (256, 128), 1) < 64
@@ -237,40 +279,39 @@
         fields = matmul(normed, wz[...]).astype(BF16)
         q, k, v = fields[:, 0:128], fields[:, 128:256], fields[:, 256:384]
         vq, pad_k = fields[:, 384:512], fields[:, 512:640]
-        m0 = matmul(weights_of(q, jnp.where(low256, k, zero256)), v)
-        m1 = matmul(weights_of(q, jnp.where(low256, zero256, k)), v)
-        m2 = matmul(weights_of(vq, pad_k), vq)
+        m0 = attend(q, jnp.where(low256, k, zero256), v)
+        m1 = attend(q, jnp.where(low256, zero256, k), v)
+        m2 = attend(vq, pad_k, vq)
         mz[:, pl.ds(r, 1), :, 0:128] = jnp.where(low256, m0, m1).reshape(32, 1, 8, 128).astype(BF16)
         mz[:, pl.ds(r, 1), :, 128:192] = m2[:, 0:64].reshape(32, 1, 8, 64).astype(BF16)
 
     def home(low, rows):
         here, there = pl.ds(low, rows), pl.ds(3 * g + low, rows)
-        local(mz.at[lon, here], h_buf.at[x, there], b_sem.at[lon]).start()
+        local(mz.at[lon, here], h_buf.at[x, there], b_sem.at[0]).start()
 
         @pl.loop(1, NX * NG)
         def _(k):
             to = lax.rem(lon + k, NX * NG)
-            remote(mz.at[to, here], h_buf.at[x, there], send.at[10], b_sem.at[lon], lat, to).start()
+            remote(mz.at[to, here], h_buf.at[x, there], send.at[10], b_sem.at[0], lat, to).start()
 
     zonal_row(0)
     home(0, 1)
-
     @pl.loop(1, 3)
     def _(r):
         zonal_row(r)
 
     home(1, 2)
 
+    hop(*packs[0])
     third(*packs[1])
     first(*packs[2])
     share(*packs[0])
+    second(*packs[2])
     settle(1, oz)
-    second(*packs[2])
     relay(*packs[1])
-
-    @pl.loop(0, NX * NG)
-    def _(k):
-        wait(h_buf.at[k // NG, pl.ds(3 * lax.rem(k, NG), 3)], b_sem.at[k])
+    third(*packs[2])
+
+    wait(h_buf, b_sem.at[0])
 
     total = tok[...].astype(F32).reshape(192, 768)
     for i in range(NX):
@@ -285,11 +326,10 @@
     s_buf[...] = by_col.reshape(8, 3, 8, 768).astype(BF16)
 
     local(s_buf.at[z], u_buf.at[yl, z], c_sem.at[lat]).start()
-    for dz in (4, 3, 5, 2, 6, 1, 7):
+    for dz in (1, 7, 2, 6, 3, 5, 4):
         to = lax.rem(z + dz, NZ)
         remote(s_buf.at[to], u_buf.at[yl, z], send.at[11], c_sem.at[lat], yl * NZ + to, lon).start()
     remote(s_buf.at[z], u_buf.at[yl, z], send.at[12], c_sem.at[lat], pair, lon).start()
-    third(*packs[2])
     for dz in (1, 7, 2, 6, 3, 5, 4):
         source = lax.rem(z + dz, NZ)
         block = u_buf.at[yl, source]
@@ -309,29 +349,26 @@
     low384 = lax.broadcasted_iota(jnp.int32, (384, 128), 1) < 64
     zero384 = jnp.zeros((384, 128), BF16)
     normed = norm(u_buf[...].astype(F32).reshape(384, 768), gm[...].reshape(1, 768))
+    fields = matmul(normed, wm[...]).astype(BF16)
     for j in range(3):
         at = 128 * j
-        q = matmul(normed, wm[:, at : at + 128]).astype(BF16)
-        k = matmul(normed, wm[:, 384 + at : 512 + at]).astype(BF16)
-        v = matmul(normed, wm[:, 768 + at : 896 + at]).astype(BF16)
-        m0 = matmul(weights_of(q, jnp.where(low384, k, zero384)), v)
-        m1 = matmul(weights_of(q, jnp.where(low384, zero384, k)), v)
+        q, k, v = (fields[:, first_at + at : first_at + at + 128] for first_at in (0, 384, 768))
+        m0 = attend(q, jnp.where(low384, k, zero384), v)
+        m1 = attend(q, jnp.where(low384, zero384, k), v)
         mm[j] = jnp.where(low384, m0, m1).reshape(16, 3, 8, 128).astype(BF16)
 
         there = h2_buf.at[yl, z, :, :, pl.ds(at, 128)]
-        local(mm.at[j, lat], there, d_sem.at[lat]).start()
+        local(mm.at[j, lat], there, d_sem.at[0]).start()
 
         @pl.loop(1, NY * NZ)
         def _(k):
             to = lax.rem(lat + k, NY * NZ)
-            remote(mm.at[j, to], there, send.at[13], d_sem.at[lat], to, lon).start()
+            remote(mm.at[j, to], there, send.at[13], d_sem.at[0], to, lon).start()
 
     share(*packs[2])
     settle(3, om)
 
-    @pl.loop(0, NY * NZ)
-    def _(k):
-        wait(h2_buf.at[k // NZ, lax.rem(k, NZ)], d_sem.at[k])
+    wait(h2_buf, d_sem.at[0])
 
     total = after[...]
     for i in range(NY):
@@ -364,10 +401,17 @@
 def body(tokens, gain_zonal, qkv_zonal, out_zonal, gain_merid, qkv_merid, out_merid):
     return pl.pallas_call(
         kernel,
-        out_shape=jax.ShapeDtypeStruct(tokens.shape, BF16),
-        in_specs=[pl.BlockSpec(memory_space=pltpu.VMEM)] * 7,
+        out_shape=pltpu.VMEM(tokens.shape, BF16),
+        in_specs=[pl.BlockSpec(memory_space=pltpu.HBM)] * 7,
         out_specs=pl.BlockSpec(memory_space=pltpu.VMEM),
         scratch_shapes=[
+            pltpu.VMEM(tokens.shape, BF16),
+            pltpu.VMEM(gain_zonal.shape, F32),
+            pltpu.VMEM(qkv_zonal.shape, BF16),
+            pltpu.VMEM(out_zonal.shape, BF16),
+            pltpu.VMEM(gain_merid.shape, F32),
+            pltpu.VMEM(qkv_merid.shape, BF16),
+            pltpu.VMEM(out_merid.shape, BF16),
             pltpu.VMEM((48, 640), BF16),
             pltpu.VMEM((2, 48, 1152), BF16),
             pltpu.VMEM((768, 640), BF16),
@@ -384,13 +428,14 @@
             pltpu.VMEM((192, 768), F32),
             pltpu.SemaphoreType.DMA((4, NY * NZ)),
             pltpu.SemaphoreType.DMA((NX * NG,)),
-            pltpu.SemaphoreType.DMA((NX * NG,)),
+            pltpu.SemaphoreType.DMA((1,)),
             pltpu.SemaphoreType.DMA((NY * NZ,)),
-            pltpu.SemaphoreType.DMA((NY * NZ,)),
+            pltpu.SemaphoreType.DMA((1,)),
             pltpu.SemaphoreType.DMA((14,)),
+            pltpu.SemaphoreType.DMA((7,)),
         ],
         compiler_params=pltpu.CompilerParams(
-            collective_id=0, has_side_effects=True, vmem_limit_bytes=56 * 1024 * 1024
+            collective_id=0, has_side_effects=True, vmem_limit_bytes=66_746_000
         ),
         name="axial",
     )(tokens, gain_zonal, qkv_zonal, out_zonal, gain_merid, qkv_merid, out_merid)

time: 83.5 us -> 79.4 us (0.951)
  Pallas kernels: 81.6 us -> 78.5 us
  local copies, waits for them, and re-layouts: 1.69 us -> 0.72 us
    pallas_call x1, Pallas kernels: 81.6 us -> 78.5 us  [body(): pl.pallas_call(kernel, out_shape=pltpu.VMEM(tokens.shape, BF16), in_specs...]
    unnamed x1, local copies, waits for them, and re-layouts: 1.69 us -> 0.72 us
where the time goes in v3:
time: 79.4 us; the launch traced here: 79.2 us
  Pallas kernels  78.5 us (99%)
    pallas_call x1, Pallas kernels, body(): pl.pallas_call(kernel, out_shape=pltpu.VMEM(tokens.shape, BF16), in_specs...  78.5 us

profile of v3, /device:TPU:1, one launch (start us, length us, event | category | flops | bytes accessed | tf_op | source)
XLA Modules:
  0.0 79.2 jit_solution(17291457622664504061)
XLA Ops:
  0.0 78.5 %axial.1 = bf16[24,8,768]{2,1,0:T(8,128)(2,1)S(1)} custom-call(bf16[24,8,768]{2,1,0:T(8,128)(2,1)} %tok_hbm.1, f32[768]{0:T(1024)} %gz_hbm.1, bf16[48,2304]{1,0:T(8,128)(2,1)} %wz_hbm.1, bf16[48,768]{1,0:T(8,128)(2,1)} %oz_hbm.1, f32[768]{0:T(1024)} %gm_hbm.1, bf16[48,2304]{1,0:T(8,128)(2,1)} %wm_hbm.1, bf16[48,768]{1,0:T(8,128)(2,1)} %om_hbm.1), custom_call_target="tpu_custom_call" | custom-call | tf_op jit(solution)/shard_map/axial/pallas_call | solution.py:402
  78.5 0.7 copy.9
